TPU v7x, 256 devices: a whole 4x4x8 slice. The times are simulated.
256 devices in a mesh: seq: 16 (over z, core), head: 4 (over x), batch: 4 (over y).
Axes of the slice: x: 4, y: 4, z: 8, core: 2. Of those that a mesh axis runs over, the one named last changes fastest.
Arguments:
- queries: bfloat16 [4, 8192, 8, 8, 128], P('batch', 'seq', 'head'), may hold values from -160 to 160
- key_rows: bfloat16 [4, 8192, 8, 128], P('batch', 'seq'), may hold values from -6 to 6
- value_rows: bfloat16 [4, 8192, 8, 128], P('batch', 'seq'), may hold values from -6 to 6
- compressed: bfloat16 [4, 128, 8, 128], P('batch', 'seq'), may hold values from -6 to 6
- chosen: int32 [4, 128, 8, 16], P('batch', 'seq'), may hold values from 0 to 127, as said below
Outputs:
- block_scores: float32 [4, 128, 8, 128], P('batch', 'seq', 'head')
- attended: bfloat16 [4, 8192, 8, 8, 128], P('batch', 'seq', 'head')
Inputs may be any that keep to these rules, and one draw needn't show every extreme that they name: `chosen`: every entry is at most its own tile number, and entry 0 of every row is the tile's own block. Over the tiles of one device of seq and one group, at most 2 different blocks of any other device are named, and every device after the first names exactly 2 blocks of the first device for each group.
All inputs are finite; a program needn't handle non-finite values.
Results may differ from a plain program's by a relative error of at most 0.008.
Values may be sent and summed in bfloat16 or wider, within the bound.
No kernel may reach another device: no remote copies, remote signals or barrier semaphores. Data moves between devices by JAX's collectives and lax.ppermute only.
A program may use at most 128 MiB of HBM per device.

v0:
```python
import jax
import jax.numpy as jnp
from jax import lax
from jax.sharding import PartitionSpec as P

HPG = 8
BLOCK = 64
TOPN = 16
CAP = 2


def laid_out(blocks, dim):
    dims = list(blocks.shape[1:])
    dims[dim] *= blocks.shape[0]
    return jnp.moveaxis(blocks, 0, dim).reshape(dims)


def copy_for_each(value, axis):
    count = lax.axis_size(axis)
    return lax.all_to_all(
        jnp.broadcast_to(value[None], (count, *value.shape)), axis, 0, 0, tiled=True
    )


def gather_directly(value, axis, dim):
    return laid_out(copy_for_each(value, axis), dim)


def cut_along(value, dim, count):
    dims = value.shape
    blocks = value.reshape(*dims[:dim], count, dims[dim] // count, *dims[dim + 1 :])
    return jnp.moveaxis(blocks, dim, 0)


def sum_at_owner(value, axis, dim):
    count = lax.axis_size(axis)
    blocks = lax.all_to_all(cut_along(value, dim, count), axis, 0, 0, tiled=True)
    return jnp.sum(blocks.astype(jnp.float32), axis=0)


def softmax_parts(scores):
    row_top = jnp.max(scores, axis=-1, keepdims=True)
    weights = jnp.exp(scores - row_top)
    return (weights, jnp.sum(weights, axis=-1, keepdims=True))


def local(queries, key_rows, value_rows, compressed, chosen):
    _, tok_rows, heads_local, groups, head_width = queries.shape
    block_len = BLOCK
    shards = lax.axis_size("seq")
    seq_rank = lax.axis_index("seq")
    blk_dev = tok_rows // block_len
    nblk = blk_dev * shards
    score_scale = head_width ** (-0.5)
    query_rows = queries[0]
    query_pos = seq_rank * tok_rows + jnp.arange(tok_rows, dtype=jnp.int32)
    logits = (
        jnp.einsum(
            "tjgd,ngd->tjgn",
            query_rows,
            gather_directly(compressed, "seq", 1)[0],
            preferred_element_type=jnp.float32,
        )
        * score_scale
    )
    all_blocks = jnp.arange(nblk, dtype=jnp.int32)
    seen = all_blocks[None, :] <= (query_pos // block_len)[:, None]
    logits = jnp.where(seen[:, None, None, :], logits, -jnp.inf)
    weights, totals = softmax_parts(logits)
    probability = weights / totals
    pooled = jnp.sum(
        probability.reshape(blk_dev, block_len, heads_local, groups, nblk), axis=(1, 2)
    )[None]
    shared = sum_at_owner(pooled.astype(jnp.bfloat16), "head", 2)
    tile_ids = seq_rank * blk_dev + jnp.arange(blk_dev, dtype=jnp.int32)
    factor = (tile_ids + 1).astype(jnp.float32) / (block_len * HPG)
    block_scores = shared * factor[None, :, None, None]
    pick_rows = chosen[0]
    onehot = pick_rows[..., None] == all_blocks
    needed = jnp.any(onehot, axis=(0, 2))
    owner_of = all_blocks // blk_dev
    needed = needed & (owner_of != seq_rank)[None, :]
    needed_grid = needed.reshape(groups, shards, blk_dev).astype(jnp.int32)
    rank_in = jnp.cumsum(needed_grid, axis=2) - needed_grid
    places = jnp.arange(CAP, dtype=jnp.int32)
    within = jnp.arange(blk_dev, dtype=jnp.int32)
    matched = (needed_grid[..., None] == 1) & (rank_in[..., None] == places)
    wanted = jnp.sum(jnp.where(matched, within[:, None], 0), axis=2)
    slot_of = blk_dev + owner_of[None, :] * CAP + rank_in.reshape(groups, nblk)
    slot_of = jnp.where(
        owner_of[None, :] == seq_rank, all_blocks[None, :] - seq_rank * blk_dev, slot_of
    )
    pool_index = jnp.sum(jnp.where(onehot, slot_of[None, :, None, :], 0), axis=3)
    key_local = key_rows[0].reshape(blk_dev, block_len, groups, head_width)
    value_local = value_rows[0].reshape(blk_dev, block_len, groups, head_width)
    group_count = groups // lax.axis_size("head")
    group_start = lax.axis_index("head") * group_count
    asked_ids = lax.dynamic_slice_in_dim(wanted, group_start, group_count, 0)
    requested = lax.all_to_all(asked_ids, "seq", split_axis=1, concat_axis=1, tiled=True)
    group_ids = group_start + jnp.arange(requested.shape[0], dtype=jnp.int32)[:, None, None]
    found = jnp.concatenate(
        [key_local[requested, :, group_ids, :], value_local[requested, :, group_ids, :]], axis=-1
    )
    fetched = lax.all_to_all(found, "seq", split_axis=1, concat_axis=1, tiled=True)
    fetched = lax.all_gather(fetched, "head", axis=0, tiled=True)
    key_remote = fetched[..., :head_width].reshape(groups, shards * CAP, block_len, head_width)
    value_remote = fetched[..., head_width:].reshape(groups, shards * CAP, block_len, head_width)
    key_pool = jnp.concatenate([jnp.transpose(key_local, (2, 0, 1, 3)), key_remote], axis=1)
    value_pool = jnp.concatenate([jnp.transpose(value_local, (2, 0, 1, 3)), value_remote], axis=1)
    tile_step = 2
    rounds = blk_dev // tile_step
    group_sel = jnp.arange(groups, dtype=jnp.int32)[None, :, None]

    def attend(inputs):
        query_part, index_part, pick_part, pos_part = inputs
        key_sel = key_pool[group_sel, index_part].reshape(
            tile_step, groups, TOPN * block_len, head_width
        )
        value_sel = value_pool[group_sel, index_part].reshape(
            tile_step, groups, TOPN * block_len, head_width
        )
        key_pos = (
            pick_part[..., None] * block_len + jnp.arange(block_len, dtype=jnp.int32)
        ).reshape(tile_step, groups, TOPN * block_len)
        scores = (
            jnp.einsum("tqhgd,tgkd->tghqk", query_part, key_sel, preferred_element_type=jnp.float32)
            * score_scale
        )
        visible = key_pos[:, :, None, None, :] <= pos_part[:, None, None, :, None]
        scores = jnp.where(visible, scores, -jnp.inf)
        weights, totals = softmax_parts(scores)
        rounded = weights.astype(jnp.bfloat16)
        mixed = jnp.einsum(
            "tghqk,tgkd->tqhgd", rounded, value_sel, preferred_element_type=jnp.float32
        )
        return (mixed / jnp.transpose(totals, (0, 3, 2, 1, 4))).astype(jnp.bfloat16)

    attended = lax.map(
        attend,
        (
            query_rows.reshape(rounds, tile_step, block_len, heads_local, groups, head_width),
            pool_index.reshape(rounds, tile_step, groups, TOPN),
            pick_rows.reshape(rounds, tile_step, groups, TOPN),
            query_pos.reshape(rounds, tile_step, block_len),
        ),
    )
    attended = attended.reshape(1, tok_rows, heads_local, groups, head_width)
    return (block_scores, attended)


def solution(mesh):
    placed = (
        P("batch", "seq", "head", None, None),
        P("batch", "seq", None, None),
        P("batch", "seq", None, None),
        P("batch", "seq", None, None),
        P("batch", "seq", None, None),
    )
    return jax.shard_map(
        local,
        mesh=mesh,
        in_specs=placed,
        out_specs=(P("batch", "seq", "head", None), P("batch", "seq", "head", None, None)),
        check_vma=False,
    )
```

profile of v0, /device:TPU:1, one launch (start us, length us, event | category | flops | bytes accessed | tf_op | source)
XLA Modules:
  0.0 301.6 jit_solution(489733168469807748)
XLA Ops:
  7.2 1.0 fusion.35
  8.3 1.3 reduce_window_sum.13
  10.6 10.0 %all-to-all-start.2 = ((s32[2,16,2]{2,0,1:T(2,128)}), s32[2,16,2]{2,0,1:T(2,128)S(1)}, u32[]{:S(2)}, u32[]{:S(2)}) async-start(s32[2,16,2]{2,0,1:T(2,128)} %copy.67), calls=%async_computation.2 | async-start | bytes 32768 | tf_op jit(solution)/shard_map/all_to_all | solution.py:99
  20.6 1.4 copy.64
  22.0 1.4 copy.63
  23.3 4.5 %all-to-all-done.2 = s32[2,16,2]{2,0,1:T(2,128)S(1)} async-done(((s32[2,16,2]{2,0,1:T(2,128)}), s32[2,16,2]{2,0,1:T(2,128)S(1)}, u32[]{:S(2)}, u32[]{:S(2)}) %all-to-all-start.2) | async-done | bytes 288 | tf_op jit(solution)/shard_map/all_to_all | solution.py:99
  29.1 1.7 gather_fusion.3
  30.8 1.6 pad_maximum_fusion.2
  32.6 53.9 %all_to_all.20 = bf16[2,16,2,64,256]{4,3,2,0,1:T(8,128)(2,1)S(1)} all-to-all(bf16[2,16,2,64,256]{4,3,2,0,1:T(8,128)(2,1)S(1)} %copy.70), channel_id=1, replica_groups=mesh['seq'=16,'head'=4,'batch'=4] {'seq'}, dimensions={1} | all-to-all | bytes 4194304 | tf_op jit(solution)/shard_map/all_to_all | solution.py:104
  86.4 1.5 copy.71
  88.7 3.4 %all-to-all-start = ((bf16[16,1,8,8,128]{4,2,3,1,0:T(8,128)(2,1)}), bf16[16,1,8,8,128]{4,2,3,1,0:T(8,128)(2,1)S(1)}, u32[]{:S(2)}, u32[]{:S(2)}) async-start(bf16[16,1,8,8,128]{4,2,3,1,0:T(8,128)(2,1)} %broadcast_in_dim.79), calls=%async_computation | async-start | bytes 524288 | tf_op jit(solution)/shard_map/all_to_all | solution.py:20
  92.4 1.3 select_reduce_fusion
  94.3 8.8 %all-to-all-done = bf16[16,1,8,8,128]{4,2,3,1,0:T(8,128)(2,1)S(1)} async-done(((bf16[16,1,8,8,128]{4,2,3,1,0:T(8,128)(2,1)}), bf16[16,1,8,8,128]{4,2,3,1,0:T(8,128)(2,1)S(1)}, u32[]{:S(2)}, u32[]{:S(2)}) %all-to-all-start) | async-done | bytes 262176 | tf_op jit(solution)/shard_map/all_to_all | solution.py:20
  103.2 3.3 %fusion.30 = f32[8,128,512,2]{2,1,3,0:T(8,128)} fusion(bf16[512,2,8,128]{3,2,1,0:T(8,128)(2,1)S(1)} %bitcast.141, bf16[16,1,8,8,128]{4,2,3,1,0:T(8,128)(2,1)S(1)} %all-to-all-done), kind=kOutput, calls=%fused_computation.45 | convolution fusion | flops 268435456 | bytes 6553600 | tf_op jit(solution)/shard_map/tjgd,ngd->tjgn/dot_general | solution.py:58
  106.5 7.5 %fusion.27 = f32[512,2,8,128]{0,3,1,2:T(8,128)} fusion(f32[8,128,512,2]{2,1,3,0:T(8,128)} %fusion.30, pred[512,128]{0,1:T(8,128)(4,1)} %iota_compare_fusion.1), kind=kOutput, calls=%fused_computation.35 | output fusion | flops 5259518 | bytes 8454144 | tf_op jit(solution)/shard_map/div | solution.py:70
  114.1 8.2 %divide_reduce_fusion = f32[512,8,128]{0,2,1:T(8,128)} fusion(f32[512,2,8,128]{0,3,1,2:T(8,128)} %fusion.27, f32[8,128,512,2]{2,1,3,0:T(8,128)} %fusion.30, pred[512,128]{0,1:T(8,128)(4,1)S(1)} %copy-done.5), kind=kOutput, calls=%fused_computation.40 | output fusion | flops 6824063 | bytes 10551296 | tf_op jit(solution)/shard_map/sub | solution.py:43
  122.3 3.0 copy.60
  125.2 1.7 bitcast_reduce_fusion
  127.6 4.0 %all-to-all-start.1 = ((bf16[4,1,8,2,128]{4,3,2,1,0:T(2,128)(2,1)}), bf16[4,1,8,2,128]{4,3,2,1,0:T(2,128)(2,1)S(1)}, u32[]{:S(2)}, u32[]{:S(2)}) async-start(bf16[4,1,8,2,128]{4,3,2,1,0:T(2,128)(2,1)} %copy.62), calls=%async_computation.1 | async-start | bytes 32768 | tf_op jit(solution)/shard_map/all_to_all | solution.py:37
  131.6 4.6 %all-to-all-done.1 = bf16[4,1,8,2,128]{4,3,2,1,0:T(2,128)(2,1)S(1)} async-done(((bf16[4,1,8,2,128]{4,3,2,1,0:T(2,128)(2,1)}), bf16[4,1,8,2,128]{4,3,2,1,0:T(2,128)(2,1)S(1)}, u32[]{:S(2)}, u32[]{:S(2)}) %all-to-all-start.1) | async-done | bytes 16416 | tf_op jit(solution)/shard_map/all_to_all | solution.py:37
  136.9 33.6 %all-gather.2.cloned.1.call-done = bf16[8,16,2,64,256]{4,3,2,1,0:T(8,128)(2,1)} async-done(((bf16[2,16,2,64,256]{4,3,2,1,0:T(8,128)(2,1)}), bf16[8,16,2,64,256]{4,3,2,1,0:T(8,128)(2,1)}) %all-gather.2.cloned.1.call-update) | async-done | bytes 8388624 | tf_op jit(solution)/shard_map/all_gather | solution.py:105
  170.5 4.5 %fusion.56 = (bf16[8,16,2,64,128]{4,3,2,1,0:T(8,128)(2,1)S(1)}, bf16[8,16,2,64,128]{4,3,2,1,0:T(8,128)(2,1)S(1)}) fusion(bf16[8,16,2,64,256]{4,3,2,1,0:T(8,128)(2,1)} %all-gather.2.cloned.1.call-done), kind=kLoop, calls=%fused_computation.102 | loop fusion | bytes 16777216 | tf_op jit(solution)/shard_map/slice | solution.py:106
  175.0 5.5 %pad_maximum_fusion = (bf16[8,40,64,128]{3,2,1,0:T(8,128)(2,1)}, bf16[8,40,64,128]{3,2,1,0:T(8,128)(2,1)}) fusion(bf16[8,32,64,128]{3,2,1,0:T(8,128)(2,1)S(1)} %bitcast.140, bf16[8,8,64,128]{3,2,1,0:T(8,128)(2,1)S(1)} %bitcast.146, bf16[8,32,64,128]{3,2,1,0:T(8,128)(2,1)S(1)} %bitcast.139, bf16[8,8,64,128]{3,2,1,0:T(8,128)(2,1)S(1)} %bitcast.144), kind=kLoop, calls=%fused_computation.37 | loop fusion | flops 5242880 | bytes 20971520 | tf_op jit(solution)/shard_map/concatenate | solution.py:109
  180.5 114.3 %while.11 = (s32[]{:T(128)}, bf16[4,2,64,2,8,128]{5,4,3,2,1,0:T(8,128)(2,1)}, s32[4,2,8,16]{3,2,1,0:T(8,128)S(1)}, bf16[8,40,64,128]{3,2,1,0:T(8,128)(2,1)}, s32...) while((s32[]{:T(128)}, ...), condition=%wide.region_12.13_spmd.clone, body=%wide.region_9.12_spmd.clone.sunk | while | flops 1098397440 | bytes 91690184 | solution.py:138
  181.6 5.8 %gather_fusion.1 = bf16[256,64,128]{2,1,0:T(8,128)(2,1)} fusion(bf16[8,40,64,128]{3,2,1,0:T(8,128)(2,1)} %get-tuple-element.213, s32[256]{0:T(256)S(1)} %reshape.360), kind=kCustom, calls=%fused_computation.1.clone.clone.1 | custom fusion | bytes 8390656 | tf_op jit(solution)/shard_map/while/body/eval_jaxpr/gather | solution.py:116
  187.4 4.1 %fusion.74 = (f32[2,8,2,64]{3,2,1,0:T(2,128)S(1)}, f32[2,8,1024,64,2]{2,3,4,1,0:T(8,128)S(1)}) fusion(pred[2,8,64,1024]{3,2,1,0:T(8,128)(4,1)S(1)} %broadcast_compare_fusion.4, bf16[2,8,1024,128,1]{3,2,4,1,0:T(8,128)(2,1)} %bitcast.138, bf16[1,2,64,2,8,128]{5,4,3,2,1,0:T(8,128)(2,1)S(1)} %constant_dynamic-slice_fusion.4), kind=kOutput, calls=%fused_computation.9.clone.1 | convolution fusion | flops 543160320 | bytes 14163968 | tf_op jit(solution)/shard_map/while/body/eval_jaxpr/tqhgd,tgkd->tghqk/dot_general | solution.py:126
  191.5 2.4 fusion.75
  194.7 5.9 %gather_fusion = bf16[256,64,128]{2,1,0:T(8,128)(2,1)} fusion(bf16[8,40,64,128]{3,2,1,0:T(8,128)(2,1)} %get-tuple-element.210, s32[256]{0:T(256)S(1)} %reshape.360), kind=kCustom, calls=%fused_computation.clone.clone.1 | custom fusion | bytes 8390656 | tf_op jit(solution)/shard_map/while/body/eval_jaxpr/gather | solution.py:119
  200.6 7.3 %fusion.76 = bf16[1,2,64,2,8,128]{5,2,3,4,1,0:T(8,128)(2,1)S(1)} fusion(bf16[2,8,1024,128,1]{3,2,4,1,0:T(8,128)(2,1)} %bitcast.137, f32[2,8,1024,64,2]{2,3,4,1,0:T(8,128)} %copy-done, f32[2,8,2,64]{3,2,1,0:T(2,128)S(1)} %get-tuple-element.188, pred[2,8,64,1024]{3,2,1,0:T(8,128)(4,1)S(1)} %broadcast_compare_fusion.4, f32[2,64,2,8]{1,2,3,0:T(2,128)S(1)} %bitcast.149), kind=kOutput, calls=%fused_computation.18.clone.1 | convolution fusion | flops 545783808 | bytes 14172160 | tf_op jit(solution)/shard_map/while/body/eval_jaxpr/tghqk,tgkd->tqhgd/dot_general | solution.py:133
  207.9 1.1 copy_dynamic-update-slice_fusion.2
  210.2 5.8 %gather_fusion.1 = bf16[256,64,128]{2,1,0:T(8,128)(2,1)} fusion(bf16[8,40,64,128]{3,2,1,0:T(8,128)(2,1)} %get-tuple-element.213, s32[256]{0:T(256)S(1)} %reshape.360), kind=kCustom, calls=%fused_computation.1.clone.clone.1 | custom fusion | bytes 8390656 | tf_op jit(solution)/shard_map/while/body/eval_jaxpr/gather | solution.py:116
  216.0 4.1 %fusion.74 = (f32[2,8,2,64]{3,2,1,0:T(2,128)S(1)}, f32[2,8,1024,64,2]{2,3,4,1,0:T(8,128)S(1)}) fusion(pred[2,8,64,1024]{3,2,1,0:T(8,128)(4,1)S(1)} %broadcast_compare_fusion.4, bf16[2,8,1024,128,1]{3,2,4,1,0:T(8,128)(2,1)} %bitcast.138, bf16[1,2,64,2,8,128]{5,4,3,2,1,0:T(8,128)(2,1)S(1)} %constant_dynamic-slice_fusion.4), kind=kOutput, calls=%fused_computation.9.clone.1 | convolution fusion | flops 543160320 | bytes 14163968 | tf_op jit(solution)/shard_map/while/body/eval_jaxpr/tqhgd,tgkd->tghqk/dot_general | solution.py:126
  220.1 2.4 fusion.75
  223.3 5.9 %gather_fusion = bf16[256,64,128]{2,1,0:T(8,128)(2,1)} fusion(bf16[8,40,64,128]{3,2,1,0:T(8,128)(2,1)} %get-tuple-element.210, s32[256]{0:T(256)S(1)} %reshape.360), kind=kCustom, calls=%fused_computation.clone.clone.1 | custom fusion | bytes 8390656 | tf_op jit(solution)/shard_map/while/body/eval_jaxpr/gather | solution.py:119
  229.2 7.3 %fusion.76 = bf16[1,2,64,2,8,128]{5,2,3,4,1,0:T(8,128)(2,1)S(1)} fusion(bf16[2,8,1024,128,1]{3,2,4,1,0:T(8,128)(2,1)} %bitcast.137, f32[2,8,1024,64,2]{2,3,4,1,0:T(8,128)} %copy-done, f32[2,8,2,64]{3,2,1,0:T(2,128)S(1)} %get-tuple-element.188, pred[2,8,64,1024]{3,2,1,0:T(8,128)(4,1)S(1)} %broadcast_compare_fusion.4, f32[2,64,2,8]{1,2,3,0:T(2,128)S(1)} %bitcast.149), kind=kOutput, calls=%fused_computation.18.clone.1 | convolution fusion | flops 545783808 | bytes 14172160 | tf_op jit(solution)/shard_map/while/body/eval_jaxpr/tghqk,tgkd->tqhgd/dot_general | solution.py:133
  236.5 1.1 copy_dynamic-update-slice_fusion.2
  238.7 5.8 %gather_fusion.1 = bf16[256,64,128]{2,1,0:T(8,128)(2,1)} fusion(bf16[8,40,64,128]{3,2,1,0:T(8,128)(2,1)} %get-tuple-element.213, s32[256]{0:T(256)S(1)} %reshape.360), kind=kCustom, calls=%fused_computation.1.clone.clone.1 | custom fusion | bytes 8390656 | tf_op jit(solution)/shard_map/while/body/eval_jaxpr/gather | solution.py:116
  244.6 4.1 %fusion.74 = (f32[2,8,2,64]{3,2,1,0:T(2,128)S(1)}, f32[2,8,1024,64,2]{2,3,4,1,0:T(8,128)S(1)}) fusion(pred[2,8,64,1024]{3,2,1,0:T(8,128)(4,1)S(1)} %broadcast_compare_fusion.4, bf16[2,8,1024,128,1]{3,2,4,1,0:T(8,128)(2,1)} %bitcast.138, bf16[1,2,64,2,8,128]{5,4,3,2,1,0:T(8,128)(2,1)S(1)} %constant_dynamic-slice_fusion.4), kind=kOutput, calls=%fused_computation.9.clone.1 | convolution fusion | flops 543160320 | bytes 14163968 | tf_op jit(solution)/shard_map/while/body/eval_jaxpr/tqhgd,tgkd->tghqk/dot_general | solution.py:126
  248.6 2.4 fusion.75
  251.9 5.9 %gather_fusion = bf16[256,64,128]{2,1,0:T(8,128)(2,1)} fusion(bf16[8,40,64,128]{3,2,1,0:T(8,128)(2,1)} %get-tuple-element.210, s32[256]{0:T(256)S(1)} %reshape.360), kind=kCustom, calls=%fused_computation.clone.clone.1 | custom fusion | bytes 8390656 | tf_op jit(solution)/shard_map/while/body/eval_jaxpr/gather | solution.py:119
  257.8 7.3 %fusion.76 = bf16[1,2,64,2,8,128]{5,2,3,4,1,0:T(8,128)(2,1)S(1)} fusion(bf16[2,8,1024,128,1]{3,2,4,1,0:T(8,128)(2,1)} %bitcast.137, f32[2,8,1024,64,2]{2,3,4,1,0:T(8,128)} %copy-done, f32[2,8,2,64]{3,2,1,0:T(2,128)S(1)} %get-tuple-element.188, pred[2,8,64,1024]{3,2,1,0:T(8,128)(4,1)S(1)} %broadcast_compare_fusion.4, f32[2,64,2,8]{1,2,3,0:T(2,128)S(1)} %bitcast.149), kind=kOutput, calls=%fused_computation.18.clone.1 | convolution fusion | flops 545783808 | bytes 14172160 | tf_op jit(solution)/shard_map/while/body/eval_jaxpr/tghqk,tgkd->tqhgd/dot_general | solution.py:133
  265.1 1.1 copy_dynamic-update-slice_fusion.2
  267.3 5.8 %gather_fusion.1 = bf16[256,64,128]{2,1,0:T(8,128)(2,1)} fusion(bf16[8,40,64,128]{3,2,1,0:T(8,128)(2,1)} %get-tuple-element.213, s32[256]{0:T(256)S(1)} %reshape.360), kind=kCustom, calls=%fused_computation.1.clone.clone.1 | custom fusion | bytes 8390656 | tf_op jit(solution)/shard_map/while/body/eval_jaxpr/gather | solution.py:116
  273.1 4.1 %fusion.74 = (f32[2,8,2,64]{3,2,1,0:T(2,128)S(1)}, f32[2,8,1024,64,2]{2,3,4,1,0:T(8,128)S(1)}) fusion(pred[2,8,64,1024]{3,2,1,0:T(8,128)(4,1)S(1)} %broadcast_compare_fusion.4, bf16[2,8,1024,128,1]{3,2,4,1,0:T(8,128)(2,1)} %bitcast.138, bf16[1,2,64,2,8,128]{5,4,3,2,1,0:T(8,128)(2,1)S(1)} %constant_dynamic-slice_fusion.4), kind=kOutput, calls=%fused_computation.9.clone.1 | convolution fusion | flops 543160320 | bytes 14163968 | tf_op jit(solution)/shard_map/while/body/eval_jaxpr/tqhgd,tgkd->tghqk/dot_general | solution.py:126
  277.2 2.4 fusion.75
  280.4 5.9 %gather_fusion = bf16[256,64,128]{2,1,0:T(8,128)(2,1)} fusion(bf16[8,40,64,128]{3,2,1,0:T(8,128)(2,1)} %get-tuple-element.210, s32[256]{0:T(256)S(1)} %reshape.360), kind=kCustom, calls=%fused_computation.clone.clone.1 | custom fusion | bytes 8390656 | tf_op jit(solution)/shard_map/while/body/eval_jaxpr/gather | solution.py:119
  286.3 7.3 %fusion.76 = bf16[1,2,64,2,8,128]{5,2,3,4,1,0:T(8,128)(2,1)S(1)} fusion(bf16[2,8,1024,128,1]{3,2,4,1,0:T(8,128)(2,1)} %bitcast.137, f32[2,8,1024,64,2]{2,3,4,1,0:T(8,128)} %copy-done, f32[2,8,2,64]{3,2,1,0:T(2,128)S(1)} %get-tuple-element.188, pred[2,8,64,1024]{3,2,1,0:T(8,128)(4,1)S(1)} %broadcast_compare_fusion.4, f32[2,64,2,8]{1,2,3,0:T(2,128)S(1)} %bitcast.149), kind=kOutput, calls=%fused_computation.18.clone.1 | convolution fusion | flops 545783808 | bytes 14172160 | tf_op jit(solution)/shard_map/while/body/eval_jaxpr/tghqk,tgkd->tqhgd/dot_general | solution.py:133
  293.6 1.1 copy_dynamic-update-slice_fusion.2
  (102 shorter events, 13.0 us)
Async XLA Ops:
  10.6 17.3 %all-to-all-start.2 = ((s32[2,16,2]{2,0,1:T(2,128)}), s32[2,16,2]{2,0,1:T(2,128)S(1)}, u32[]{:S(2)}, u32[]{:S(2)}) async-start(s32[2,16,2]{2,0,1:T(2,128)} %copy.67), calls=%async_computation.2 | async-start | bytes 32768 | tf_op jit(solution)/shard_map/all_to_all | solution.py:99
  20.5 149.9 %all-gather.2.cloned.1.call-start = ((), (), s32[]{:S(2)}) async-start(), calls=%async_computation.4 | async-start | bytes 10485760 | tf_op jit(solution)/shard_map/all_gather | solution.py:105
  23.3 9.0 %copy-start.2 = (bf16[1,512,8,128]{3,1,2,0:T(8,128)(2,1)}, bf16[1,512,8,128]{3,1,2,0:T(8,128)(2,1)S(1)}, u32[]{:S(2)}) copy-start(bf16[1,512,8,128]{3,1,2,0:T(8,128)(2,1)S(1)} %copy.63) | copy-start | bytes 3145732
  86.4 1.5 copy-start.6
  86.4 5.9 %copy-start.4 = (s32[1,8,8,16]{3,2,1,0:T(8,128)S(1)}, s32[1,8,8,16]{3,2,1,0:T(8,128)}, u32[]{:S(2)}) copy-start(s32[1,8,8,16]{3,2,1,0:T(8,128)} %param.11) | copy-start | bytes 12292
  86.4 16.7 %copy-start.1 = (bf16[1,512,2,8,128]{4,3,2,1,0:T(8,128)(2,1)S(1)}, bf16[1,512,2,8,128]{4,3,2,1,0:T(8,128)(2,1)}, u32[]{:S(2)}) copy-start(bf16[1,512,2,8,128]{4,3,2,1,0:T(8,128)(2,1)} %param.7) | copy-start | bytes 6291460
  88.7 14.4 %all-to-all-start = ((bf16[16,1,8,8,128]{4,2,3,1,0:T(8,128)(2,1)}), bf16[16,1,8,8,128]{4,2,3,1,0:T(8,128)(2,1)S(1)}, u32[]{:S(2)}, u32[]{:S(2)}) async-start(bf16[16,1,8,8,128]{4,2,3,1,0:T(8,128)(2,1)} %broadcast_in_dim.79), calls=%async_computation | async-start | bytes 524288 | tf_op jit(solution)/shard_map/all_to_all | solution.py:20
  106.5 7.6 %copy-start.5 = (pred[512,128]{0,1:T(8,128)(4,1)S(1)}, pred[512,128]{0,1:T(8,128)(4,1)}, u32[]{:S(2)}) copy-start(pred[512,128]{0,1:T(8,128)(4,1)} %iota_compare_fusion.1) | copy-start | bytes 196612
  127.6 8.6 %all-to-all-start.1 = ((bf16[4,1,8,2,128]{4,3,2,1,0:T(2,128)(2,1)}), bf16[4,1,8,2,128]{4,3,2,1,0:T(2,128)(2,1)S(1)}, u32[]{:S(2)}, u32[]{:S(2)}) async-start(bf16[4,1,8,2,128]{4,3,2,1,0:T(2,128)(2,1)} %copy.62), calls=%async_computation.1 | async-start | bytes 32768 | tf_op jit(solution)/shard_map/all_to_all | solution.py:37
  170.5 4.5 %copy-start.3 = (bf16[1,512,8,128]{3,1,2,0:T(8,128)(2,1)S(1)}, bf16[1,512,8,128]{3,1,2,0:T(8,128)(2,1)}, u32[]{:S(2)}) copy-start(bf16[1,512,8,128]{3,1,2,0:T(8,128)(2,1)} %copy-done.2) | copy-start | bytes 3145732
  191.5 3.2 %copy-start = (f32[2,8,1024,64,2]{2,3,4,1,0:T(8,128)}, f32[2,8,1024,64,2]{2,3,4,1,0:T(8,128)S(1)}, u32[]{:S(2)}) copy-start(f32[2,8,1024,64,2]{2,3,4,1,0:T(8,128)S(1)} %get-tuple-element.187) | copy-start | bytes 25165828 | tf_op jit(solution)/shard_map/while
  220.1 3.2 %copy-start = (f32[2,8,1024,64,2]{2,3,4,1,0:T(8,128)}, f32[2,8,1024,64,2]{2,3,4,1,0:T(8,128)S(1)}, u32[]{:S(2)}) copy-start(f32[2,8,1024,64,2]{2,3,4,1,0:T(8,128)S(1)} %get-tuple-element.187) | copy-start | bytes 25165828 | tf_op jit(solution)/shard_map/while
  248.6 3.2 %copy-start = (f32[2,8,1024,64,2]{2,3,4,1,0:T(8,128)}, f32[2,8,1024,64,2]{2,3,4,1,0:T(8,128)S(1)}, u32[]{:S(2)}) copy-start(f32[2,8,1024,64,2]{2,3,4,1,0:T(8,128)S(1)} %get-tuple-element.187) | copy-start | bytes 25165828 | tf_op jit(solution)/shard_map/while
  277.2 3.2 %copy-start = (f32[2,8,1024,64,2]{2,3,4,1,0:T(8,128)}, f32[2,8,1024,64,2]{2,3,4,1,0:T(8,128)S(1)}, u32[]{:S(2)}) copy-start(f32[2,8,1024,64,2]{2,3,4,1,0:T(8,128)S(1)} %get-tuple-element.187) | copy-start | bytes 25165828 | tf_op jit(solution)/shard_map/while
Sparse Core Ops, SparseCore 0:
  88.1 82.3 all-gather.1
where the time goes:
time: 303 us; the launch traced here: 302 us
  local copies, waits for them, and re-layouts  73.2 us (24%)
  blocking collectives  53.9 us (18%)
  waiting for transfers between devices  51.5 us (17%)
  matrix products  48.7 us (16%)
  other arithmetic  42.3 us (14%)
  starting transfers between devices  17.4 us (6%)
  between operations  14.3 us (5%)
    all_to_all x1, blocking collectives, local(): lax.all_to_all(found, 'seq', split_axis=1, concat_axis=1, tiled=True)  53.9 us
    all_gather x1, waiting for transfers between devices, local(): fetched = lax.all_gather(fetched, 'head', axis=0, tiled=True)  33.6 us
    dot_general x4, matrix products, attend(): jnp.einsum('tghqk,tgkd->tqhgd', rounded, value_sel, preferred_element_typ...  29.2 us
    gather x4, local copies, waits for them, and re-layouts, attend(): value_pool[group_sel, index_part]  23.6 us
    gather x4, local copies, waits for them, and re-layouts, attend(): key_pool[group_sel, index_part]  23.2 us
    dot_general x4, matrix products, attend(): jnp.einsum('tqhgd,tgkd->tghqk', query_part, key_sel, preferred_element_ty...  16.2 us
    all_to_all x1, starting transfers between devices, local(): lax.all_to_all(asked_ids, 'seq', split_axis=1, concat_axis=1, tiled=True)  9.97 us
    reduce_sum x4, other arithmetic, softmax_parts(): return (weights, jnp.sum(weights, axis=-1, keepdims=True))  9.72 us
  transfers between devices with their start and end apart: 4, of which 4 were waited for; matrix products, arithmetic and copies ran while one was open for 10% of the time, Pallas kernels for 0%

commit v1 on v0

--- a/solution.py
+++ b/solution.py
@@ -102,7 +102,9 @@
         [key_local[requested, :, group_ids, :], value_local[requested, :, group_ids, :]], axis=-1
     )
     fetched = lax.all_to_all(found, "seq", split_axis=1, concat_axis=1, tiled=True)
-    fetched = lax.all_gather(fetched, "head", axis=0, tiled=True)
+    fetched = jnp.concatenate(
+        lax.all_to_all(jnp.stack([fetched] * lax.axis_size("head")), "head", 0, 0), axis=0
+    )
     key_remote = fetched[..., :head_width].reshape(groups, shards * CAP, block_len, head_width)
     value_remote = fetched[..., head_width:].reshape(groups, shards * CAP, block_len, head_width)
     key_pool = jnp.concatenate([jnp.transpose(key_local, (2, 0, 1, 3)), key_remote], axis=1)

time: 303 us -> 329 us (1.086)
  waiting for transfers between devices: 51.5 us -> 125 us
  blocking collectives: 53.9 us -> 0 us
  between operations: 14.3 us -> 0.88 us
  starting transfers between devices: 17.4 us -> 28 us
  local copies, waits for them, and re-layouts: 73.2 us -> 82 us
    all_to_all x0 -> x2, waiting for transfers between devices: none -> 114 us  [the longest x1 89.4 us: local(): lax.all_to_all(jnp.stack([fetched] * lax.axis_size('head')), 'head', 0, 0)]
    all_to_all x1 -> x0, blocking collectives: 53.9 us -> none  [local(): lax.all_to_all(found, 'seq', split_axis=1, concat_axis=1, tiled=True)]
    all_gather x1 -> x0, waiting for transfers between devices: 33.6 us -> none  [local(): fetched = lax.all_gather(fetched, 'head', axis=0, tiled=True)]
    all_to_all x0 -> x2, starting transfers between devices: none -> 10.3 us  [the longest x1 5.96 us: local(): lax.all_to_all(jnp.stack([fetched] * lax.axis_size('head')), 'head', 0, 0)]
    another operation x0 -> x1, local copies, waits for them, and re-layouts: none -> 5.89 us  [local(): jnp.stack([fetched] * lax.axis_size('head'))]
    all_to_all x1, waiting for transfers between devices: 4.56 us -> 1.05 us  [sum_at_owner(): lax.all_to_all(cut_along(value, dim, count), axis, 0, 0, tiled=True)]
  transfers between devices with their start and end apart: 4 -> 5, of which waited for: 4 -> 5; matrix products, arithmetic and copies ran while one was open for 10% -> 12% of each run, Pallas kernels for 0% -> 0%
where the time goes in v1:
time: 329 us; the launch traced here: 326 us
  waiting for transfers between devices  125 us (38%)
  local copies, waits for them, and re-layouts  82 us (25%)
  matrix products  48.7 us (15%)
  other arithmetic  41.2 us (13%)
  starting transfers between devices  28 us (9%)
    all_to_all x1, waiting for transfers between devices, local(): lax.all_to_all(jnp.stack([fetched] * lax.axis_size('head')), 'head', 0, 0)  89.4 us
    dot_general x4, matrix products, attend(): jnp.einsum('tghqk,tgkd->tqhgd', rounded, value_sel, preferred_element_typ...  29.2 us
    all_to_all x1, waiting for transfers between devices, local(): lax.all_to_all(found, 'seq', split_axis=1, concat_axis=1, tiled=True)  24.2 us
    gather x4, local copies, waits for them, and re-layouts, attend(): value_pool[group_sel, index_part]  23.6 us
    gather x4, local copies, waits for them, and re-layouts, attend(): key_pool[group_sel, index_part]  23.2 us
    dot_general x4, matrix products, attend(): jnp.einsum('tqhgd,tgkd->tghqk', query_part, key_sel, preferred_element_ty...  16.2 us
    all_to_all x1, starting transfers between devices, local(): lax.all_to_all(asked_ids, 'seq', split_axis=1, concat_axis=1, tiled=True)  9.97 us
    reduce_sum x4, other arithmetic, softmax_parts(): return (weights, jnp.sum(weights, axis=-1, keepdims=True))  9.72 us
  transfers between devices with their start and end apart: 5, of which 5 were waited for; matrix products, arithmetic and copies ran while one was open for 12% of the time, Pallas kernels for 0%

profile of v1, /device:TPU:1, one launch (start us, length us, event | category | flops | bytes accessed | tf_op | source)
XLA Modules:
  0.0 326.0 jit_solution(16692509521807975946)
XLA Ops:
  1.8 1.3 reduce_window_sum.13
  4.0 10.0 %all-to-all-start.2 = ((s32[2,16,2]{2,0,1:T(2,128)}), s32[2,16,2]{2,0,1:T(2,128)S(1)}, u32[]{:S(2)}, u32[]{:S(2)}) async-start(s32[2,16,2]{2,0,1:T(2,128)} %copy.67), calls=%async_computation.2 | async-start | bytes 32768 | tf_op jit(solution)/shard_map/all_to_all | solution.py:99
  14.0 1.4 copy.64
  15.4 1.4 copy.63
  16.8 4.6 %all-to-all-done.2 = s32[2,16,2]{2,0,1:T(2,128)S(1)} async-done(((s32[2,16,2]{2,0,1:T(2,128)}), s32[2,16,2]{2,0,1:T(2,128)S(1)}, u32[]{:S(2)}, u32[]{:S(2)}) %all-to-all-start.2) | async-done | bytes 288 | tf_op jit(solution)/shard_map/all_to_all | solution.py:99
  22.1 3.7 %all-to-all-start = ((bf16[16,1,8,8,128]{4,2,3,1,0:T(8,128)(2,1)}), bf16[16,1,8,8,128]{4,2,3,1,0:T(8,128)(2,1)S(1)}, u32[]{:S(2)}, u32[]{:S(2)}) async-start(bf16[16,1,8,8,128]{4,2,3,1,0:T(8,128)(2,1)} %broadcast_in_dim.79), calls=%async_computation | async-start | bytes 524288 | tf_op jit(solution)/shard_map/all_to_all | solution.py:20
  27.0 1.7 gather_fusion.3
  28.7 1.6 pad_maximum_fusion.2
  30.3 1.5 copy.70
  31.8 5.8 %all-to-all-done = bf16[16,1,8,8,128]{4,2,3,1,0:T(8,128)(2,1)S(1)} async-done(((bf16[16,1,8,8,128]{4,2,3,1,0:T(8,128)(2,1)}), bf16[16,1,8,8,128]{4,2,3,1,0:T(8,128)(2,1)S(1)}, u32[]{:S(2)}, u32[]{:S(2)}) %all-to-all-start) | async-done | bytes 262176 | tf_op jit(solution)/shard_map/all_to_all | solution.py:20
  37.6 4.3 %all-to-all-start.3 = ((bf16[2,16,2,64,256]{4,3,2,0,1:T(8,128)(2,1)}), bf16[2,16,2,64,256]{4,3,2,0,1:T(8,128)(2,1)}, u32[]{:S(2)}, u32[]{:S(2)}) async-start(bf16[2,16,2,64,256]{4,3,2,0,1:T(8,128)(2,1)} %copy.70), calls=%async_computation.3 | async-start | bytes 4194304 | tf_op jit(solution)/shard_map/all_to_all | solution.py:104
  42.0 3.3 %fusion.30 = f32[8,128,512,2]{2,1,3,0:T(8,128)} fusion(bf16[512,2,8,128]{3,2,1,0:T(8,128)(2,1)S(1)} %bitcast.142, bf16[16,1,8,8,128]{4,2,3,1,0:T(8,128)(2,1)S(1)} %all-to-all-done), kind=kOutput, calls=%fused_computation.45 | convolution fusion | flops 268435456 | bytes 6553600 | tf_op jit(solution)/shard_map/tjgd,ngd->tjgn/dot_general | solution.py:58
  45.3 7.3 %fusion.27 = f32[512,2,8,128]{0,3,1,2:T(8,128)} fusion(f32[8,128,512,2]{2,1,3,0:T(8,128)} %fusion.30, pred[512,128]{0,1:T(8,128)(4,1)S(1)} %iota_compare_fusion.1), kind=kOutput, calls=%fused_computation.35 | output fusion | flops 5259518 | bytes 8454144 | tf_op jit(solution)/shard_map/div | solution.py:70
  52.6 8.0 %divide_reduce_fusion = f32[512,8,128]{0,2,1:T(8,128)} fusion(f32[512,2,8,128]{0,3,1,2:T(8,128)} %fusion.27, f32[8,128,512,2]{2,1,3,0:T(8,128)} %fusion.30, pred[512,128]{0,1:T(8,128)(4,1)S(1)} %iota_compare_fusion.1), kind=kOutput, calls=%fused_computation.40 | output fusion | flops 6824063 | bytes 10551296 | tf_op jit(solution)/shard_map/sub | solution.py:43
  60.6 3.0 copy.60
  63.6 1.7 bitcast_reduce_fusion
  65.9 24.2 %all-to-all-done.3 = bf16[2,16,2,64,256]{4,3,2,0,1:T(8,128)(2,1)} async-done(((bf16[2,16,2,64,256]{4,3,2,0,1:T(8,128)(2,1)}), bf16[2,16,2,64,256]{4,3,2,0,1:T(8,128)(2,1)}, u32[]{:S(2)}, u32[]{:S(2)}) %all-to-all-start.3) | async-done | bytes 2097184 | tf_op jit(solution)/shard_map/all_to_all | solution.py:104
  90.0 4.0 %all-to-all-start.1 = ((bf16[4,1,8,2,128]{4,3,2,1,0:T(2,128)(2,1)}), bf16[4,1,8,2,128]{4,3,2,1,0:T(2,128)(2,1)S(1)}, u32[]{:S(2)}, u32[]{:S(2)}) async-start(bf16[4,1,8,2,128]{4,3,2,1,0:T(2,128)(2,1)} %copy.62), calls=%async_computation.1 | async-start | bytes 32768 | tf_op jit(solution)/shard_map/all_to_all | solution.py:37
  94.1 3.2 copy.71
  98.3 5.9 %stack.2 = bf16[4,2,16,2,64,256]{5,4,3,2,1,0:T(8,128)(2,1)} broadcast(bf16[2,16,2,64,256]{4,3,2,1,0:T(8,128)(2,1)} %copy.71), dimensions={1,2,3,4,5} | broadcast | bytes 10485760 | tf_op jit(solution)/shard_map/stack | solution.py:106
  104.2 6.0 %all-to-all-start.4 = ((bf16[4,2,16,2,64,256]{5,4,3,2,1,0:T(8,128)(2,1)}), bf16[4,2,16,2,64,256]{5,4,3,2,1,0:T(8,128)(2,1)}, u32[]{:S(2)}, u32[]{:S(2)}) async-start(bf16[4,2,16,2,64,256]{5,4,3,2,1,0:T(8,128)(2,1)} %stack.2), calls=%async_computation.4 | async-start | bytes 16777216 | tf_op jit(solution)/shard_map/all_to_all | solution.py:106
  110.3 1.3 select_reduce_fusion
  112.3 89.4 %all-to-all-done.4 = bf16[4,2,16,2,64,256]{5,4,3,2,1,0:T(8,128)(2,1)} async-done(((bf16[4,2,16,2,64,256]{5,4,3,2,1,0:T(8,128)(2,1)}), bf16[4,2,16,2,64,256]{5,4,3,2,1,0:T(8,128)(2,1)}, u32[]{:S(2)}, u32[]{:S(2)}) %all-to-all-start.4) | async-done | bytes 8388640 | tf_op jit(solution)/shard_map/all_to_all | solution.py:106
  201.7 4.5 %fusion.56 = (bf16[8,16,2,64,128]{4,3,2,1,0:T(8,128)(2,1)S(1)}, bf16[8,16,2,64,128]{4,3,2,1,0:T(8,128)(2,1)S(1)}) fusion(bf16[8,16,2,64,256]{4,3,2,1,0:T(8,128)(2,1)} %bitcast.18), kind=kLoop, calls=%fused_computation.102 | loop fusion | bytes 16777216 | tf_op jit(solution)/shard_map/slice | solution.py:108
  206.3 5.5 %pad_maximum_fusion = (bf16[8,40,64,128]{3,2,1,0:T(8,128)(2,1)}, bf16[8,40,64,128]{3,2,1,0:T(8,128)(2,1)}) fusion(bf16[8,32,64,128]{3,2,1,0:T(8,128)(2,1)S(1)} %bitcast.141, bf16[8,8,64,128]{3,2,1,0:T(8,128)(2,1)S(1)} %bitcast.147, bf16[8,32,64,128]{3,2,1,0:T(8,128)(2,1)S(1)} %bitcast.140, bf16[8,8,64,128]{3,2,1,0:T(8,128)(2,1)S(1)} %bitcast.145), kind=kLoop, calls=%fused_computation.37 | loop fusion | flops 5242880 | bytes 20971520 | tf_op jit(solution)/shard_map/concatenate | solution.py:111
  211.7 114.3 %while.11 = (s32[]{:T(128)}, bf16[4,2,64,2,8,128]{5,4,3,2,1,0:T(8,128)(2,1)}, s32[4,2,8,16]{3,2,1,0:T(8,128)S(1)}, bf16[8,40,64,128]{3,2,1,0:T(8,128)(2,1)}, s32...) while((s32[]{:T(128)}, ...), condition=%wide.region_12.13_spmd.clone, body=%wide.region_9.12_spmd.clone.sunk | while | flops 1098397440 | bytes 91690184 | solution.py:140
  212.9 5.8 %gather_fusion.1 = bf16[256,64,128]{2,1,0:T(8,128)(2,1)} fusion(bf16[8,40,64,128]{3,2,1,0:T(8,128)(2,1)} %get-tuple-element.213, s32[256]{0:T(256)S(1)} %reshape.366), kind=kCustom, calls=%fused_computation.1.clone.clone.1 | custom fusion | bytes 8390656 | tf_op jit(solution)/shard_map/while/body/eval_jaxpr/gather | solution.py:118
  218.7 4.1 %fusion.74 = (f32[2,8,2,64]{3,2,1,0:T(2,128)S(1)}, f32[2,8,1024,64,2]{2,3,4,1,0:T(8,128)S(1)}) fusion(pred[2,8,64,1024]{3,2,1,0:T(8,128)(4,1)S(1)} %broadcast_compare_fusion.4, bf16[2,8,1024,128,1]{3,2,4,1,0:T(8,128)(2,1)} %bitcast.139, bf16[1,2,64,2,8,128]{5,4,3,2,1,0:T(8,128)(2,1)S(1)} %constant_dynamic-slice_fusion.4), kind=kOutput, calls=%fused_computation.9.clone.1 | convolution fusion | flops 543160320 | bytes 14163968 | tf_op jit(solution)/shard_map/while/body/eval_jaxpr/tqhgd,tgkd->tghqk/dot_general | solution.py:128
  222.8 2.4 fusion.75
  226.0 5.9 %gather_fusion = bf16[256,64,128]{2,1,0:T(8,128)(2,1)} fusion(bf16[8,40,64,128]{3,2,1,0:T(8,128)(2,1)} %get-tuple-element.210, s32[256]{0:T(256)S(1)} %reshape.366), kind=kCustom, calls=%fused_computation.clone.clone.1 | custom fusion | bytes 8390656 | tf_op jit(solution)/shard_map/while/body/eval_jaxpr/gather | solution.py:121
  231.9 7.3 %fusion.76 = bf16[1,2,64,2,8,128]{5,2,3,4,1,0:T(8,128)(2,1)S(1)} fusion(bf16[2,8,1024,128,1]{3,2,4,1,0:T(8,128)(2,1)} %bitcast.138, f32[2,8,1024,64,2]{2,3,4,1,0:T(8,128)} %copy-done, f32[2,8,2,64]{3,2,1,0:T(2,128)S(1)} %get-tuple-element.188, pred[2,8,64,1024]{3,2,1,0:T(8,128)(4,1)S(1)} %broadcast_compare_fusion.4, f32[2,64,2,8]{1,2,3,0:T(2,128)S(1)} %bitcast.150), kind=kOutput, calls=%fused_computation.18.clone.1 | convolution fusion | flops 545783808 | bytes 14172160 | tf_op jit(solution)/shard_map/while/body/eval_jaxpr/tghqk,tgkd->tqhgd/dot_general | solution.py:135
  239.2 1.1 copy_dynamic-update-slice_fusion.2
  241.4 5.8 %gather_fusion.1 = bf16[256,64,128]{2,1,0:T(8,128)(2,1)} fusion(bf16[8,40,64,128]{3,2,1,0:T(8,128)(2,1)} %get-tuple-element.213, s32[256]{0:T(256)S(1)} %reshape.366), kind=kCustom, calls=%fused_computation.1.clone.clone.1 | custom fusion | bytes 8390656 | tf_op jit(solution)/shard_map/while/body/eval_jaxpr/gather | solution.py:118
  247.3 4.1 %fusion.74 = (f32[2,8,2,64]{3,2,1,0:T(2,128)S(1)}, f32[2,8,1024,64,2]{2,3,4,1,0:T(8,128)S(1)}) fusion(pred[2,8,64,1024]{3,2,1,0:T(8,128)(4,1)S(1)} %broadcast_compare_fusion.4, bf16[2,8,1024,128,1]{3,2,4,1,0:T(8,128)(2,1)} %bitcast.139, bf16[1,2,64,2,8,128]{5,4,3,2,1,0:T(8,128)(2,1)S(1)} %constant_dynamic-slice_fusion.4), kind=kOutput, calls=%fused_computation.9.clone.1 | convolution fusion | flops 543160320 | bytes 14163968 | tf_op jit(solution)/shard_map/while/body/eval_jaxpr/tqhgd,tgkd->tghqk/dot_general | solution.py:128
  251.3 2.4 fusion.75
  254.6 5.9 %gather_fusion = bf16[256,64,128]{2,1,0:T(8,128)(2,1)} fusion(bf16[8,40,64,128]{3,2,1,0:T(8,128)(2,1)} %get-tuple-element.210, s32[256]{0:T(256)S(1)} %reshape.366), kind=kCustom, calls=%fused_computation.clone.clone.1 | custom fusion | bytes 8390656 | tf_op jit(solution)/shard_map/while/body/eval_jaxpr/gather | solution.py:121
  260.5 7.3 %fusion.76 = bf16[1,2,64,2,8,128]{5,2,3,4,1,0:T(8,128)(2,1)S(1)} fusion(bf16[2,8,1024,128,1]{3,2,4,1,0:T(8,128)(2,1)} %bitcast.138, f32[2,8,1024,64,2]{2,3,4,1,0:T(8,128)} %copy-done, f32[2,8,2,64]{3,2,1,0:T(2,128)S(1)} %get-tuple-element.188, pred[2,8,64,1024]{3,2,1,0:T(8,128)(4,1)S(1)} %broadcast_compare_fusion.4, f32[2,64,2,8]{1,2,3,0:T(2,128)S(1)} %bitcast.150), kind=kOutput, calls=%fused_computation.18.clone.1 | convolution fusion | flops 545783808 | bytes 14172160 | tf_op jit(solution)/shard_map/while/body/eval_jaxpr/tghqk,tgkd->tqhgd/dot_general | solution.py:135
  267.7 1.1 copy_dynamic-update-slice_fusion.2
  270.0 5.8 %gather_fusion.1 = bf16[256,64,128]{2,1,0:T(8,128)(2,1)} fusion(bf16[8,40,64,128]{3,2,1,0:T(8,128)(2,1)} %get-tuple-element.213, s32[256]{0:T(256)S(1)} %reshape.366), kind=kCustom, calls=%fused_computation.1.clone.clone.1 | custom fusion | bytes 8390656 | tf_op jit(solution)/shard_map/while/body/eval_jaxpr/gather | solution.py:118
  275.8 4.1 %fusion.74 = (f32[2,8,2,64]{3,2,1,0:T(2,128)S(1)}, f32[2,8,1024,64,2]{2,3,4,1,0:T(8,128)S(1)}) fusion(pred[2,8,64,1024]{3,2,1,0:T(8,128)(4,1)S(1)} %broadcast_compare_fusion.4, bf16[2,8,1024,128,1]{3,2,4,1,0:T(8,128)(2,1)} %bitcast.139, bf16[1,2,64,2,8,128]{5,4,3,2,1,0:T(8,128)(2,1)S(1)} %constant_dynamic-slice_fusion.4), kind=kOutput, calls=%fused_computation.9.clone.1 | convolution fusion | flops 543160320 | bytes 14163968 | tf_op jit(solution)/shard_map/while/body/eval_jaxpr/tqhgd,tgkd->tghqk/dot_general | solution.py:128
  279.9 2.4 fusion.75
  283.1 5.9 %gather_fusion = bf16[256,64,128]{2,1,0:T(8,128)(2,1)} fusion(bf16[8,40,64,128]{3,2,1,0:T(8,128)(2,1)} %get-tuple-element.210, s32[256]{0:T(256)S(1)} %reshape.366), kind=kCustom, calls=%fused_computation.clone.clone.1 | custom fusion | bytes 8390656 | tf_op jit(solution)/shard_map/while/body/eval_jaxpr/gather | solution.py:121
  289.0 7.3 %fusion.76 = bf16[1,2,64,2,8,128]{5,2,3,4,1,0:T(8,128)(2,1)S(1)} fusion(bf16[2,8,1024,128,1]{3,2,4,1,0:T(8,128)(2,1)} %bitcast.138, f32[2,8,1024,64,2]{2,3,4,1,0:T(8,128)} %copy-done, f32[2,8,2,64]{3,2,1,0:T(2,128)S(1)} %get-tuple-element.188, pred[2,8,64,1024]{3,2,1,0:T(8,128)(4,1)S(1)} %broadcast_compare_fusion.4, f32[2,64,2,8]{1,2,3,0:T(2,128)S(1)} %bitcast.150), kind=kOutput, calls=%fused_computation.18.clone.1 | convolution fusion | flops 545783808 | bytes 14172160 | tf_op jit(solution)/shard_map/while/body/eval_jaxpr/tghqk,tgkd->tqhgd/dot_general | solution.py:135
  298.6 5.8 %gather_fusion.1 = bf16[256,64,128]{2,1,0:T(8,128)(2,1)} fusion(bf16[8,40,64,128]{3,2,1,0:T(8,128)(2,1)} %get-tuple-element.213, s32[256]{0:T(256)S(1)} %reshape.366), kind=kCustom, calls=%fused_computation.1.clone.clone.1 | custom fusion | bytes 8390656 | tf_op jit(solution)/shard_map/while/body/eval_jaxpr/gather | solution.py:118
  304.4 4.1 %fusion.74 = (f32[2,8,2,64]{3,2,1,0:T(2,128)S(1)}, f32[2,8,1024,64,2]{2,3,4,1,0:T(8,128)S(1)}) fusion(pred[2,8,64,1024]{3,2,1,0:T(8,128)(4,1)S(1)} %broadcast_compare_fusion.4, bf16[2,8,1024,128,1]{3,2,4,1,0:T(8,128)(2,1)} %bitcast.139, bf16[1,2,64,2,8,128]{5,4,3,2,1,0:T(8,128)(2,1)S(1)} %constant_dynamic-slice_fusion.4), kind=kOutput, calls=%fused_computation.9.clone.1 | convolution fusion | flops 543160320 | bytes 14163968 | tf_op jit(solution)/shard_map/while/body/eval_jaxpr/tqhgd,tgkd->tghqk/dot_general | solution.py:128
  308.5 2.4 fusion.75
  311.7 5.9 %gather_fusion = bf16[256,64,128]{2,1,0:T(8,128)(2,1)} fusion(bf16[8,40,64,128]{3,2,1,0:T(8,128)(2,1)} %get-tuple-element.210, s32[256]{0:T(256)S(1)} %reshape.366), kind=kCustom, calls=%fused_computation.clone.clone.1 | custom fusion | bytes 8390656 | tf_op jit(solution)/shard_map/while/body/eval_jaxpr/gather | solution.py:121
  317.6 7.3 %fusion.76 = bf16[1,2,64,2,8,128]{5,2,3,4,1,0:T(8,128)(2,1)S(1)} fusion(bf16[2,8,1024,128,1]{3,2,4,1,0:T(8,128)(2,1)} %bitcast.138, f32[2,8,1024,64,2]{2,3,4,1,0:T(8,128)} %copy-done, f32[2,8,2,64]{3,2,1,0:T(2,128)S(1)} %get-tuple-element.188, pred[2,8,64,1024]{3,2,1,0:T(8,128)(4,1)S(1)} %broadcast_compare_fusion.4, f32[2,64,2,8]{1,2,3,0:T(2,128)S(1)} %bitcast.150), kind=kOutput, calls=%fused_computation.18.clone.1 | convolution fusion | flops 545783808 | bytes 14172160 | tf_op jit(solution)/shard_map/while/body/eval_jaxpr/tghqk,tgkd->tqhgd/dot_general | solution.py:135
  (101 shorter events, 16.4 us)
Async XLA Ops:
  0.6 16.1 %copy-start.5 = (bf16[1,8,8,128]{3,2,1,0:T(8,128)(2,1)S(1)}, bf16[1,8,8,128]{3,2,1,0:T(8,128)(2,1)}, u32[]{:S(2)}) copy-start(bf16[1,8,8,128]{3,2,1,0:T(8,128)(2,1)} %param.10) | copy-start | bytes 49156
  4.0 17.3 %all-to-all-start.2 = ((s32[2,16,2]{2,0,1:T(2,128)}), s32[2,16,2]{2,0,1:T(2,128)S(1)}, u32[]{:S(2)}, u32[]{:S(2)}) async-start(s32[2,16,2]{2,0,1:T(2,128)} %copy.67), calls=%async_computation.2 | async-start | bytes 32768 | tf_op jit(solution)/shard_map/all_to_all | solution.py:99
  16.8 12.0 %copy-start.2 = (bf16[1,512,8,128]{3,1,2,0:T(8,128)(2,1)}, bf16[1,512,8,128]{3,1,2,0:T(8,128)(2,1)S(1)}, u32[]{:S(2)}) copy-start(bf16[1,512,8,128]{3,1,2,0:T(8,128)(2,1)S(1)} %copy.63) | copy-start | bytes 3145732
  22.1 15.5 %all-to-all-start = ((bf16[16,1,8,8,128]{4,2,3,1,0:T(8,128)(2,1)}), bf16[16,1,8,8,128]{4,2,3,1,0:T(8,128)(2,1)S(1)}, u32[]{:S(2)}, u32[]{:S(2)}) async-start(bf16[16,1,8,8,128]{4,2,3,1,0:T(8,128)(2,1)} %broadcast_in_dim.79), calls=%async_computation | async-start | bytes 524288 | tf_op jit(solution)/shard_map/all_to_all | solution.py:20
  30.3 11.7 %copy-start.1 = (bf16[1,512,2,8,128]{4,3,2,1,0:T(8,128)(2,1)S(1)}, bf16[1,512,2,8,128]{4,3,2,1,0:T(8,128)(2,1)}, u32[]{:S(2)}) copy-start(bf16[1,512,2,8,128]{4,3,2,1,0:T(8,128)(2,1)} %param.7) | copy-start | bytes 6291460
  37.6 52.5 %all-to-all-start.3 = ((bf16[2,16,2,64,256]{4,3,2,0,1:T(8,128)(2,1)}), bf16[2,16,2,64,256]{4,3,2,0,1:T(8,128)(2,1)}, u32[]{:S(2)}, u32[]{:S(2)}) async-start(bf16[2,16,2,64,256]{4,3,2,0,1:T(8,128)(2,1)} %copy.70), calls=%async_computation.3 | async-start | bytes 4194304 | tf_op jit(solution)/shard_map/all_to_all | solution.py:104
  90.0 8.2 %all-to-all-start.1 = ((bf16[4,1,8,2,128]{4,3,2,1,0:T(2,128)(2,1)}), bf16[4,1,8,2,128]{4,3,2,1,0:T(2,128)(2,1)S(1)}, u32[]{:S(2)}, u32[]{:S(2)}) async-start(bf16[4,1,8,2,128]{4,3,2,1,0:T(2,128)(2,1)} %copy.62), calls=%async_computation.1 | async-start | bytes 32768 | tf_op jit(solution)/shard_map/all_to_all | solution.py:37
  104.2 6.2 %copy-start.4 = (s32[1,8,8,16]{3,2,1,0:T(8,128)S(1)}, s32[1,8,8,16]{3,2,1,0:T(8,128)}, u32[]{:S(2)}) copy-start(s32[1,8,8,16]{3,2,1,0:T(8,128)} %param.11) | copy-start | bytes 12292
  104.2 97.6 %all-to-all-start.4 = ((bf16[4,2,16,2,64,256]{5,4,3,2,1,0:T(8,128)(2,1)}), bf16[4,2,16,2,64,256]{5,4,3,2,1,0:T(8,128)(2,1)}, u32[]{:S(2)}, u32[]{:S(2)}) async-start(bf16[4,2,16,2,64,256]{5,4,3,2,1,0:T(8,128)(2,1)} %stack.2), calls=%async_computation.4 | async-start | bytes 16777216 | tf_op jit(solution)/shard_map/all_to_all | solution.py:106
  201.7 4.5 %copy-start.3 = (bf16[1,512,8,128]{3,1,2,0:T(8,128)(2,1)S(1)}, bf16[1,512,8,128]{3,1,2,0:T(8,128)(2,1)}, u32[]{:S(2)}) copy-start(bf16[1,512,8,128]{3,1,2,0:T(8,128)(2,1)} %copy-done.2) | copy-start | bytes 3145732
  222.8 3.2 copy-start
  251.3 3.2 copy-start
  279.9 3.2 copy-start
  308.5 3.2 copy-start
